TPU v7x, 128 devices: a whole 4x4x4 slice. The times are simulated.
128 devices in a mesh: dp: 128 (over x, z, y, core).
Axes of the slice: x: 4, y: 4, z: 4, core: 2. Of those that a mesh axis runs over, the one named last changes fastest.
Arguments:
- grads: float32 [128, 8192, 128], P('dp'), may hold values from -6 to 6
- error: float32 [128, 8192, 128], P('dp'), may hold values from -4 to 4
- picks: int32 [128, 32], P('dp'), may hold values from 0 to 8191, as said below
- owned_ids: int32 [8192], P('dp'), may hold values from 0 to 8191, as said below
- params: float32 [8192, 128], P('dp'), may hold values from -6 to 6
- momentum: float32 [8192, 128], P('dp'), may hold values from -6 to 6
Outputs:
- new_error: float32 [128, 8192, 128], P('dp')
- new_params: float32 [8192, 128], P('dp')
- new_momentum: float32 [8192, 128], P('dp')
Inputs may be any that keep to these rules, and one draw needn't show every extreme that they name: `picks`: each row holds 32 different block numbers; at most 4 of a row's blocks lie in the slots of one device, and one device's slots hold exactly 4 blocks of every row. `owned_ids`: every block number appears once.
All inputs are finite; a program needn't handle non-finite values.
Results may differ from a plain program's by a relative error of at most 0.000064.
Values sent between devices are 32-bit elements; how exact they have to be, the bound alone decides.
No kernel may reach another device: no remote copies, remote signals or barrier semaphores. Data moves between devices by JAX's collectives and lax.ppermute only.
A program may use at most 64 MiB of HBM per device.

v0:
```python
import jax
import jax.numpy as jnp
from jax import lax
from jax.sharding import Mesh
from jax.sharding import PartitionSpec as P

DP = ("dp_0", "dp_1", "dp_2", "dp_3")


def from_everyone(x, axis):
    peers = lax.axis_size(axis)
    return lax.all_to_all(jnp.broadcast_to(x[None], (peers, *x.shape)), axis, 0, 0, tiled=True)


def joined_along(pieces, dim):
    pieces = jnp.moveaxis(pieces, 0, dim)
    shape = pieces.shape
    return pieces.reshape(*shape[:dim], shape[dim] * shape[dim + 1], *shape[dim + 2 :])


def gather_axes(x, axes, dim):
    far, near = axes
    first = from_everyone(x, far)
    pieces = jnp.swapaxes(from_everyone(first, near), 0, 1)
    return joined_along(pieces.reshape(-1, *x.shape), dim)


def on_device(grads, error, picks, owned_ids, params, momentum):
    acc = grads[0] + error[0]
    blocks = acc.shape[0]
    own_rows = params.shape[0]
    chosen = picks[0]
    keep = jnp.zeros((blocks,), jnp.float32).at[chosen].set(1.0)
    new_error = (acc * (1.0 - keep)[:, None])[None]
    all_owned = gather_axes(owned_ids, (("dp_0", "dp_1", "dp_2"), "dp_3"), 0)
    slot_range = jnp.arange(own_rows, dtype=jnp.int32)
    inverse = jnp.zeros((blocks,), jnp.int32).at[all_owned].set(jnp.arange(blocks, dtype=jnp.int32))
    ndev = lax.axis_size(DP)
    count = chosen.shape[0]
    limit = min(4, count)
    slot_of = jnp.take(inverse, chosen, axis=0)
    owner = slot_of // own_rows
    local = slot_of - owner * own_rows
    order_idx = jnp.arange(count, dtype=jnp.int32)
    earlier = (owner[:, None] == owner[None, :]) & (order_idx[None, :] < order_idx[:, None])
    position = jnp.sum(earlier.astype(jnp.int32), axis=1)
    target = owner * limit + position
    send_values = (
        jnp.zeros((ndev * limit, acc.shape[1]), jnp.float32)
        .at[target]
        .set(jnp.take(acc, chosen, axis=0))
    )
    send_slots = jnp.full((ndev * limit,), -1, jnp.int32).at[target].set(local)
    got_values, got_slots = (
        lax.all_to_all(send_values, DP, split_axis=0, concat_axis=0, tiled=True),
        lax.all_to_all(send_slots, DP, split_axis=0, concat_axis=0, tiled=True),
    )
    onehot = (got_slots[:, None] == slot_range[None, :]).astype(jnp.float32)
    owned_total = lax.dot_general(
        onehot,
        got_values,
        (((0,), (0,)), ((), ())),
        precision=lax.Precision.HIGHEST,
        preferred_element_type=jnp.float32,
    )
    new_momentum = 0.9 * momentum + owned_total
    new_params = params - 0.5 * new_momentum
    return (new_error, new_params, new_momentum)


def solution(mesh):
    split = Mesh(mesh.devices.reshape(4, 4, 4, 2), ("dp_0", "dp_1", "dp_2", "dp_3"))
    return jax.shard_map(
        on_device,
        mesh=split,
        in_specs=(
            P(DP, None, None),
            P(DP, None, None),
            P(DP, None),
            P(DP),
            P(DP, None),
            P(DP, None),
        ),
        out_specs=(P(DP, None, None), P(DP, None), P(DP, None)),
        check_vma=False,
    )
```

profile of v0, /device:TPU:1, one launch (start us, length us, event | category | flops | bytes accessed | tf_op | source)
XLA Modules:
  0.0 98.1 jit_solution(16543489616717990210)
XLA Ops:
  0.6 1.3 %broadcast_in_dim.61 = s32[64,1,64]{2,1,0:T(1,128)} broadcast(s32[64]{0:T(128)} %param.9), dimensions={2} | broadcast | bytes 16640 | tf_op jit(solution)/shard_map/broadcast_in_dim | solution.py:12
  1.9 12.0 %all-to-all-start = ((s32[64,1,64]{2,1,0:T(1,128)}), s32[64,1,64]{2,1,0:T(1,128)S(1)}, u32[]{:S(2)}, u32[]{:S(2)}) async-start(s32[64,1,64]{2,1,0:T(1,128)} %broadcast_in_dim.61), calls=%async_computation | async-start | bytes 65536 | tf_op jit(solution)/shard_map/all_to_all | solution.py:12
  13.9 0.7 fusion.16
  14.5 0.7 scatter_custom_fusion
  15.3 6.9 %all-to-all-done = s32[64,1,64]{2,1,0:T(1,128)S(1)} async-done(((s32[64,1,64]{2,1,0:T(1,128)}), s32[64,1,64]{2,1,0:T(1,128)S(1)}, u32[]{:S(2)}, u32[]{:S(2)}) %all-to-all-start) | async-done | bytes 16416 | tf_op jit(solution)/shard_map/all_to_all | solution.py:12
  22.2 0.1 reshape.262
  22.3 5.5 %all_to_all.32 = s32[2,1,4096]{2,1,0:T(1,128)S(1)} all-to-all(s32[2,1,4096]{2,1,0:T(1,128)S(1)} %reshape.262), channel_id=1, replica_groups=mesh['dp_0'=4,'dp_1'=4,'dp_2'=4,'dp_3'=2] {'dp_3'}, dimensions={0} | all-to-all | bytes 65536 | tf_op jit(solution)/shard_map/all_to_all | solution.py:12
  27.8 0.5 broadcast.235
  28.4 0.7 reduce.4
  29.1 0.1 reshape.263
  29.2 0.1 copy.11
  29.3 0.1 reshape_reshape.3
  29.4 30.5 %scatter_custom_fusion.1 = s32[8192]{0:T(1024)S(1)} fusion(s32[8192]{0:T(1024)S(1)} %bitcast.40, s32[8192]{0:T(1024)S(1)} %iota.14, s32[]{:T(128)} %constant.28.clone.1), kind=kCustom, calls=%fused_computation.18 | custom fusion | bytes 32772 | tf_op jit(solution)/shard_map/scatter | solution.py:37
  59.9 0.7 gather_fusion
  60.6 0.7 fusion.14
  61.3 0.7 multiply_subtract_fusion.1
  62.0 0.2 convert_reduce_fusion
  62.1 0.7 fusion.13
  62.8 0.7 scatter_custom_fusion.2
  63.5 0.7 all_to_all.23
  64.2 3.9 %all-to-all-start.2 = ((s32[128,4,1]{1,2,0:T(1,128)}), s32[128,4,1]{1,2,0:T(1,128)S(1)}, u32[]{:S(2)}, u32[]{:S(2)}) async-start(s32[128,4,1]{1,2,0:T(1,128)} %bitcast.11), calls=%async_computation.2 | async-start | bytes 131072 | tf_op jit(solution)/shard_map/all_to_all | solution.py:56
  68.1 6.1 %add_bitcast_fusion = (f32[8192,128]{1,0:T(8,128)}, f32[1,8192,128]{2,1,0:T(8,128)}) fusion(f32[1,8192,128]{2,1,0:T(8,128)} %param.6, f32[1,8192,128]{2,1,0:T(8,128)} %param.7, f32[8192]{0:T(1024)S(1)} %broadcast_subtract_fusion), kind=kLoop, calls=%fused_computation.7 | loop fusion | flops 2097152 | bytes 16809984 | tf_op jit(solution)/shard_map/add | solution.py:29
  74.2 2.2 %scatter_custom_fusion.3 = f32[512,128]{1,0:T(8,128)} fusion(s32[32]{0:T(128)S(1)} %fusion.13, f32[]{:T(128)} %constant.21.clone.1, f32[]{:T(128)} %constant.64.clone.1, pred[32]{0:T(512)(128)(4,1)S(1)} %get-tuple-element.5, f32[8192,128]{1,0:T(8,128)} %get-tuple-element.6, s32[1024]{0:T(1024)S(1)} %pad_clamp_fusion), kind=kCustom, calls=%fused_computation.11 | custom fusion | flops 4096 | bytes 4461064 | tf_op jit(solution)/shard_map/scatter | solution.py:51
  76.4 1.2 %all-to-all-done.2 = s32[128,4,1]{1,2,0:T(1,128)S(1)} async-done(((s32[128,4,1]{1,2,0:T(1,128)}), s32[128,4,1]{1,2,0:T(1,128)S(1)}, u32[]{:S(2)}, u32[]{:S(2)}) %all-to-all-start.2) | async-done | bytes 2080 | tf_op jit(solution)/shard_map/all_to_all | solution.py:56
  77.6 8.6 %all-to-all-start.3 = ((f32[128,4,128]{2,1,0:T(4,128)}), f32[128,4,128]{2,1,0:T(4,128)S(1)}, u32[]{:S(2)}, u32[]{:S(2)}) async-start(f32[128,4,128]{2,1,0:T(4,128)} %bitcast.13), calls=%async_computation.3 | async-start | bytes 524288 | tf_op jit(solution)/shard_map/all_to_all | solution.py:55
  86.2 0.5 broadcast.232
  86.7 0.8 reduce.3
  87.5 0.1 eq.34
  87.6 9.4 %all-to-all-done.3 = f32[128,4,128]{2,1,0:T(4,128)S(1)} async-done(((f32[128,4,128]{2,1,0:T(4,128)}), f32[128,4,128]{2,1,0:T(4,128)S(1)}, u32[]{:S(2)}, u32[]{:S(2)}) %all-to-all-start.3) | async-done | bytes 262176 | tf_op jit(solution)/shard_map/all_to_all | solution.py:55
  97.0 0.0 copy-done
  97.0 0.0 copy-done.1
  97.0 1.1 %multiply_subtract_fusion = (f32[64,128]{1,0:T(8,128)}, f32[64,128]{1,0:T(8,128)}) fusion(f32[64,128]{1,0:T(8,128)S(1)} %copy-done, f32[512,128]{1,0:T(8,128)S(1)} %bitcast.37, s32[512]{0:T(512)S(1)} %eq.34, f32[64,128]{1,0:T(8,128)S(1)} %copy-done.1), kind=kOutput, calls=%fused_computation.14 | convolution fusion | flops 50397184 | bytes 395264 | tf_op jit(solution)/shard_map/dot_general | solution.py:59
  (8 shorter events, 0.1 us)
Async XLA Ops:
  1.9 20.3 %all-to-all-start = ((s32[64,1,64]{2,1,0:T(1,128)}), s32[64,1,64]{2,1,0:T(1,128)S(1)}, u32[]{:S(2)}, u32[]{:S(2)}) async-start(s32[64,1,64]{2,1,0:T(1,128)} %broadcast_in_dim.61), calls=%async_computation | async-start | bytes 65536 | tf_op jit(solution)/shard_map/all_to_all | solution.py:12
  64.2 13.4 %all-to-all-start.2 = ((s32[128,4,1]{1,2,0:T(1,128)}), s32[128,4,1]{1,2,0:T(1,128)S(1)}, u32[]{:S(2)}, u32[]{:S(2)}) async-start(s32[128,4,1]{1,2,0:T(1,128)} %bitcast.11), calls=%async_computation.2 | async-start | bytes 131072 | tf_op jit(solution)/shard_map/all_to_all | solution.py:56
  74.2 22.8 %copy-start = (f32[64,128]{1,0:T(8,128)S(1)}, f32[64,128]{1,0:T(8,128)}, u32[]{:S(2)}) copy-start(f32[64,128]{1,0:T(8,128)} %param.10) | copy-start | bytes 98308
  74.2 22.8 %copy-start.1 = (f32[64,128]{1,0:T(8,128)S(1)}, f32[64,128]{1,0:T(8,128)}, u32[]{:S(2)}) copy-start(f32[64,128]{1,0:T(8,128)} %param.11) | copy-start | bytes 98308
  77.6 19.4 %all-to-all-start.3 = ((f32[128,4,128]{2,1,0:T(4,128)}), f32[128,4,128]{2,1,0:T(4,128)S(1)}, u32[]{:S(2)}, u32[]{:S(2)}) async-start(f32[128,4,128]{2,1,0:T(4,128)} %bitcast.13), calls=%async_computation.3 | async-start | bytes 524288 | tf_op jit(solution)/shard_map/all_to_all | solution.py:55
where the time goes:
time: 98.4 us; the launch traced here: 98.1 us
  local copies, waits for them, and re-layouts  36.1 us (37%)
  starting transfers between devices  24.4 us (25%)
  waiting for transfers between devices  17.5 us (18%)
  other arithmetic  12.7 us (13%)
  blocking collectives  5.51 us (6%)
  matrix products  1.09 us (1%)
    scatter x1, local copies, waits for them, and re-layouts, on_device(): jnp.zeros((blocks,), jnp.int32).at[all_owned]  30.5 us
    all_to_all x1, starting transfers between devices, from_everyone(): lax.all_to_all(jnp.broadcast_to(x[None], (peers, *x.shape)), axis, 0, 0,...  12 us
    all_to_all x1, waiting for transfers between devices, on_device(): lax.all_to_all(send_values, DP, split_axis=0, concat_axis=0, tiled=True)  9.37 us
    all_to_all x1, starting transfers between devices, on_device(): lax.all_to_all(send_values, DP, split_axis=0, concat_axis=0, tiled=True)  8.55 us
    all_to_all x1, waiting for transfers between devices, from_everyone(): lax.all_to_all(jnp.broadcast_to(x[None], (peers, *x.shape)), axis, 0, 0,...  6.94 us
    add x1, other arithmetic, on_device(): acc = grads[0] + error[0]  6.1 us
    all_to_all x1, blocking collectives, from_everyone(): lax.all_to_all(jnp.broadcast_to(x[None], (peers, *x.shape)), axis, 0, 0,...  5.51 us
    all_to_all x1, starting transfers between devices, on_device(): lax.all_to_all(send_slots, DP, split_axis=0, concat_axis=0, tiled=True)  3.88 us
  transfers between devices with their start and end apart: 3, of which 3 were waited for; matrix products, arithmetic and copies ran while one was open for 11% of the time, Pallas kernels for 0%

commit v1 on v0

v1 whole, which is shorter than its diff:
```python
import jax
import jax.numpy as jnp
from jax import lax
from jax.experimental import pallas as pl
from jax.experimental.pallas import tpu as pltpu
from jax.sharding import Mesh
from jax.sharding import PartitionSpec as P

DP = ("x", "z", "yh", "yl", "c")
GATHER = ("x", "z", "yh")
SERVE = ("yl", "c")
PEERS = 32
LANES = 128
STEP = 1024


def xor_pairs(bits):
    return [(i, i ^ bits) for i in range(4)]


def rows_kernel(picks_hbm, grads, error, out, picks, gbuf, ebuf, psem, gsem, esem):
    fetch = pltpu.make_async_copy(picks_hbm, picks, psem)
    fetch.start()
    fetch.wait()
    count = picks.shape[0]
    for k in range(count):
        row = picks[k]
        pltpu.make_async_copy(grads.at[pl.ds(row, 1)], gbuf.at[pl.ds(k, 1)], gsem).start()
        pltpu.make_async_copy(error.at[pl.ds(row, 1)], ebuf.at[pl.ds(k, 1)], esem).start()
    lane = lax.broadcasted_iota(jnp.int32, (1, LANES), 1) % count
    ids = jnp.zeros((1, LANES), jnp.int32)
    for k in range(count):
        ids = jnp.where(lane == k, picks[k], ids)
    pltpu.make_async_copy(grads.at[pl.ds(0, count)], gbuf, gsem).wait()
    pltpu.make_async_copy(error.at[pl.ds(0, count)], ebuf, esem).wait()
    acc = gbuf[:, 0, :] + ebuf[:, 0, :]
    ids = ids.astype(jnp.float32)
    for p in range(PEERS):
        base = p * (count + 1)
        out[base : base + count, :] = acc
        out[base + count : base + count + 1, :] = ids


def chosen_rows(picks, grads, error):
    count = picks.shape[0]
    return pl.pallas_call(
        rows_kernel,
        in_specs=[pl.BlockSpec(memory_space=pltpu.HBM)] * 3,
        scratch_shapes=[
            pltpu.SMEM((count,), jnp.int32),
            pltpu.VMEM((count, 1, LANES), jnp.float32),
            pltpu.VMEM((count, 1, LANES), jnp.float32),
            pltpu.SemaphoreType.DMA,
            pltpu.SemaphoreType.DMA,
            pltpu.SemaphoreType.DMA,
        ],
        out_shape=jax.ShapeDtypeStruct((PEERS * (count + 1), LANES), jnp.float32),
        name="chosen_rows",
    )(picks, grads.reshape(-1, 1, LANES), error.reshape(-1, 1, LANES))


def dense_kernel(picks, grads, error, out):
    out[...] = grads[...] + error[...]
    start = pl.program_id(0) * STEP
    for k in range(picks.shape[0]):
        row = picks[k] - start

        @pl.when((row >= 0) & (row < STEP))
        def _():
            out[pl.ds(row, 1), :] = jnp.zeros((1, LANES), jnp.float32)


def remainder(picks, grads, error):
    blocks = grads.shape[0]
    spec = pl.BlockSpec((STEP, LANES), lambda i, p: (i, 0))
    return pl.pallas_call(
        dense_kernel,
        grid_spec=pltpu.PrefetchScalarGridSpec(
            num_scalar_prefetch=1,
            grid=(blocks // STEP,),
            in_specs=[spec, spec],
            out_specs=spec,
        ),
        out_shape=jax.ShapeDtypeStruct(grads.shape, jnp.float32),
        cost_estimate=pl.CostEstimate(
            flops=40_000_000, bytes_accessed=12 << 20, transcendentals=0
        ),
        name="remainder",
    )(picks, grads, error)


def totals_kernel(got, id0, id1, id2, id3, out0, out1, out2, out3):
    count = got.shape[0] // PEERS - 1
    per = LANES // count
    lane = lax.broadcasted_iota(jnp.int32, (1, LANES), 1)
    slots = id0.shape[1]
    columns = []
    for ids in (id0, id1, id2, id3):
        wide = jnp.broadcast_to(ids[...].astype(jnp.float32), (LANES, slots))
        columns.append(wide.T)
    owned = jnp.concatenate(columns, axis=0)
    marks, values = [], []
    for g in range(PEERS // per):
        ids = None
        for q in range(per):
            base = (g * per + q) * (count + 1)
            row = got[base + count : base + count + 1, :]
            ids = row if ids is None else jnp.where(lane < q * count, ids, row)
            values.append(got[base : base + count, :])
        marks.append(jnp.where(owned == ids, 1.0, 0.0).astype(jnp.bfloat16))
    marks = jnp.concatenate(marks, axis=1)
    values = jnp.concatenate(values, axis=0)
    total = None
    for _ in range(3):
        part = values.astype(jnp.bfloat16)
        values = values - part.astype(jnp.float32)
        term = jnp.dot(marks, part, preferred_element_type=jnp.float32)
        total = term if total is None else total + term
    for j, out in enumerate((out0, out1, out2, out3)):
        out[...] = total[j * slots : (j + 1) * slots, :]


def totals(got, ids):
    slots = ids[0].shape[1]
    return pl.pallas_call(
        totals_kernel,
        out_shape=[jax.ShapeDtypeStruct((slots, LANES), jnp.float32)] * 4,
        compiler_params=pltpu.CompilerParams(vmem_limit_bytes=8 << 20),
        name="totals",
    )(got, *ids)


def update_kernel(momentum, params, a, b, c, d, new_params, new_momentum):
    fresh = 0.9 * momentum[...] + ((a[...] + b[...]) + (c[...] + d[...]))
    new_momentum[...] = fresh
    new_params[...] = params[...] - 0.5 * fresh


def update(momentum, params, parts):
    shape = jax.ShapeDtypeStruct(params.shape, jnp.float32)
    return pl.pallas_call(
        update_kernel,
        out_shape=[shape, shape],
        compiler_params=pltpu.CompilerParams(vmem_limit_bytes=2 << 20),
        name="update",
    )(momentum, params, *parts)


def on_device(grads, error, picks, owned_ids, params, momentum):
    grads, error, picks = grads[0], error[0], picks[0]
    count = picks.shape[0]
    send = chosen_rows(picks, grads, error)
    send = send.reshape(PEERS, count + 1, 1, LANES)
    got = lax.all_to_all(send, GATHER, 0, 0, tiled=True)
    mine = owned_ids.reshape(1, -1)
    ids = [mine] + [lax.ppermute(mine, SERVE, xor_pairs(b)) for b in (1, 2, 3)]
    new_error = remainder(picks, grads, error)
    got, new_error = lax.optimization_barrier((got, new_error))
    parts = totals(got.reshape(-1, LANES), ids)
    parts = [parts[0]] + [lax.ppermute(parts[b], SERVE, xor_pairs(b)) for b in (1, 2, 3)]
    new_params, new_momentum = update(momentum, params, parts)
    return new_error[None], new_params, new_momentum


def solution(mesh):
    split = Mesh(mesh.devices.reshape(4, 4, 2, 2, 2), DP)
    return jax.shard_map(
        on_device,
        mesh=split,
        in_specs=(
            P(DP, None, None),
            P(DP, None, None),
            P(DP, None),
            P(DP),
            P(DP, None),
            P(DP, None),
        ),
        out_specs=(P(DP, None, None), P(DP, None), P(DP, None)),
        check_vma=False,
    )
```

time: 98.4 us -> 35.3 us (0.36)
  local copies, waits for them, and re-layouts: 36.1 us -> 0.01 us
  waiting for transfers between devices: 17.5 us -> 3.08 us
  Pallas kernels: 0 us -> 13.3 us
  other arithmetic: 12.7 us -> 0 us
  starting transfers between devices: 24.4 us -> 17.7 us
  blocking collectives: 5.51 us -> 0 us
  matrix products: 1.09 us -> 0 us
    scatter x3 -> x0, local copies, waits for them, and re-layouts: 31.9 us -> none  [the longest x1 30.5 us: on_device(): jnp.zeros((blocks,), jnp.int32).at[all_owned]]
    all_to_all x3 -> x1, waiting for transfers between devices: 17.5 us -> 0.74 us  [on_device(): got = lax.all_to_all(send, GATHER, 0, 0, tiled=True)]
    pallas_call x0 -> x4, Pallas kernels: none -> 13.3 us  [the longest x1 9.32 us: remainder(): pl.pallas_call(dense_kernel, grid_spec=pltpu.PrefetchScalarGridSpec(num_s...]
    all_to_all x3 -> x1, starting transfers between devices: 24.4 us -> 11.3 us  [on_device(): got = lax.all_to_all(send, GATHER, 0, 0, tiled=True)]
    ppermute x0 -> x6, starting transfers between devices: none -> 6.4 us  [the longest x3 4.01 us: on_device(): lax.ppermute(parts[b], SERVE, xor_pairs(b))]
    add x1 -> x0, other arithmetic: 6.1 us -> none  [on_device(): acc = grads[0] + error[0]]
    all_to_all x1 -> x0, blocking collectives: 5.51 us -> none  [from_everyone(): lax.all_to_all(jnp.broadcast_to(x[None], (peers, *x.shape)), axis, 0, 0,...]
    ppermute x0 -> x6, waiting for transfers between devices: none -> 2.34 us  [the longest x3 2.34 us: on_device(): lax.ppermute(parts[b], SERVE, xor_pairs(b))]
  transfers between devices with their start and end apart: 3 -> 7, of which waited for: 3 -> 3; matrix products, arithmetic and copies ran while one was open for 11% -> 0% of each run, Pallas kernels for 0% -> 27%
where the time goes in v1:
time: 35.3 us; the launch traced here: 34.8 us
  starting transfers between devices  17.7 us (50%)
  Pallas kernels  13.3 us (38%)
  waiting for transfers between devices  3.08 us (9%)
  between operations  0.68 us (2%)
    all_to_all x1, starting transfers between devices, on_device(): got = lax.all_to_all(send, GATHER, 0, 0, tiled=True)  11.3 us
    pallas_call x1, Pallas kernels, remainder(): pl.pallas_call(dense_kernel, grid_spec=pltpu.PrefetchScalarGridSpec(num_s...  9.32 us
    ppermute x3, starting transfers between devices, on_device(): lax.ppermute(parts[b], SERVE, xor_pairs(b))  4.01 us
    pallas_call x1, Pallas kernels, chosen_rows(): pl.pallas_call(rows_kernel, in_specs=[pl.BlockSpec(memory_space=pltpu.HBM...  2.7 us
    ppermute x3, starting transfers between devices, on_device(): ids = [mine] + [lax.ppermute(mine, SERVE, xor_pairs(b)) for b in (1, 2, 3)]  2.39 us
    ppermute x3, waiting for transfers between devices, on_device(): lax.ppermute(parts[b], SERVE, xor_pairs(b))  2.34 us
    all_to_all x1, waiting for transfers between devices, on_device(): got = lax.all_to_all(send, GATHER, 0, 0, tiled=True)  0.74 us
  transfers between devices with their start and end apart: 7, of which 3 were waited for; matrix products, arithmetic and copies ran while one was open for 0% of the time, Pallas kernels for 27%

profile of v1, /device:TPU:1, one launch (start us, length us, event | category | flops | bytes accessed | tf_op | source)
XLA Modules:
  0.0 34.8 jit_solution(17372402435110130988)
XLA Ops:
  0.6 0.0 copy-start.2
  0.6 2.7 %chosen_rows.1 = f32[1056,128]{1,0:T(8,128)} custom-call(s32[32]{0:T(128)} %bitcast.20, f32[8192,1,128]{2,1,0:T(1,128)} %bitcast.14, f32[8192,1,128]{2,1,0:T(1,128)} %bitcast.16), custom_call_target="tpu_custom_call" | custom-call | tf_op jit(solution)/shard_map/chosen_rows/pallas_call | solution.py:46
  3.3 11.3 %all-to-all-start = ((f32[32,33,1,128]{3,2,1,0:T(1,128)}), f32[32,33,1,128]{3,2,1,0:T(1,128)S(1)}, u32[]{:S(2)}, u32[]{:S(2)}) async-start(f32[32,33,1,128]{3,2,1,0:T(1,128)} %bitcast.19), calls=%async_computation | async-start | bytes 1081344 | tf_op jit(solution)/shard_map/all_to_all | solution.py:154
  14.7 0.0 copy-done.2
  14.7 1.3 %collective-permute-start.2 = (s32[1,64]{1,0:T(1,128)S(1)}, s32[1,64]{1,0:T(1,128)S(1)}, u32[]{:S(2)}, u32[]{:S(2)}) collective-permute-start(s32[1,64]{1,0:T(1,128)S(1)} %bitcast.10), channel_id=1, source_target_pairs={{0,3},{1,2},{2,1},{3,0},{4,7},{5,6},{6,5},{7,4},{8,11},{9,10},{10,... | collective-permute-start | bytes 776 | tf_op jit(solution)/shard_map/ppermute | solution.py:156
  16.0 1.1 %collective-permute-start.1 = (s32[1,64]{1,0:T(1,128)S(1)}, s32[1,64]{1,0:T(1,128)S(1)}, u32[]{:S(2)}, u32[]{:S(2)}) collective-permute-start(s32[1,64]{1,0:T(1,128)S(1)} %bitcast.11), channel_id=1, source_target_pairs={{0,2},{1,3},{2,0},{3,1},{4,6},{5,7},{6,4},{7,5},{8,10},{9,11},{10,... | collective-permute-start | bytes 776 | tf_op jit(solution)/shard_map/ppermute | solution.py:156
  17.1 0.0 collective-permute-start
  17.1 0.0 copy-start
  17.1 0.0 copy-start.1
  17.1 9.3 %remainder.1 = f32[8192,128]{1,0:T(8,128)} custom-call(s32[32]{0:T(128)} %bitcast.21, f32[8192,128]{1,0:T(8,128)} %bitcast.15, f32[8192,128]{1,0:T(8,128)} %bitcast.17), custom_call_target="tpu_custom_call" | custom-call | flops 40000000 | bytes 12582912 | tf_op jit(solution)/shard_map/remainder/pallas_call | solution.py:76
  26.4 0.7 %all-to-all-done = f32[32,33,1,128]{3,2,1,0:T(1,128)S(1)} async-done(((f32[32,33,1,128]{3,2,1,0:T(1,128)}), f32[32,33,1,128]{3,2,1,0:T(1,128)S(1)}, u32[]{:S(2)}, u32[]{:S(2)}) %all-to-all-start) | async-done | bytes 540704 | tf_op jit(solution)/shard_map/all_to_all | solution.py:154
  27.2 0.0 collective-permute-done.2.id3
  27.2 0.0 collective-permute-done.1.id2
  27.2 0.0 collective-permute-done.id1
  27.2 0.6 %totals.1 = (f32[64,128]{1,0:T(8,128)S(1)}, f32[64,128]{1,0:T(8,128)S(1)}, f32[64,128]{1,0:T(8,128)S(1)}, f32[64,128]{1,0:T(8,128)S(1)}) custom-call(f32[1056,128]{1,0:T(8,128)S(1)} %bitcast.9, s32[1,64]{1,0:T(1,128)S(1)} %bitcast.13, s32[1,64]{1,0:T(1,128)S(1)} %collective-permute-done.id1, s32[1,64]{1,0:T(1,128)S(1)} %collective-permute-done.1.id2, ...), custom_call_target="tpu_custom_call" | custom-call | tf_op jit(solution)/shard_map/totals/pallas_call | solution.py:125
  27.8 2.3 %collective-permute-start.3 = (f32[64,128]{1,0:T(8,128)S(1)}, f32[64,128]{1,0:T(8,128)S(1)}, u32[]{:S(2)}, u32[]{:S(2)}) collective-permute-start(f32[64,128]{1,0:T(8,128)S(1)} %get-tuple-element.14), channel_id=1, source_target_pairs={{0,1},{1,0},{2,3},{3,2},{4,5},{5,4},{6,7},{7,6},{8,9},{9,8},{10,11... | collective-permute-start | bytes 98312 | tf_op jit(solution)/shard_map/ppermute | solution.py:160
  30.1 0.4 %collective-permute-start.4 = (f32[64,128]{1,0:T(8,128)S(1)}, f32[64,128]{1,0:T(8,128)S(1)}, u32[]{:S(2)}, u32[]{:S(2)}) collective-permute-start(f32[64,128]{1,0:T(8,128)S(1)} %get-tuple-element.15), channel_id=1, source_target_pairs={{0,2},{1,3},{2,0},{3,1},{4,6},{5,7},{6,4},{7,5},{8,10},{9,11},{10,... | collective-permute-start | bytes 98312 | tf_op jit(solution)/shard_map/ppermute | solution.py:160
  30.5 1.3 %collective-permute-start.5 = (f32[64,128]{1,0:T(8,128)S(1)}, f32[64,128]{1,0:T(8,128)S(1)}, u32[]{:S(2)}, u32[]{:S(2)}) collective-permute-start(f32[64,128]{1,0:T(8,128)S(1)} %get-tuple-element.16), channel_id=1, source_target_pairs={{0,3},{1,2},{2,1},{3,0},{4,7},{5,6},{6,5},{7,4},{8,11},{9,10},{10,... | collective-permute-start | bytes 98312 | tf_op jit(solution)/shard_map/ppermute | solution.py:160
  31.8 0.0 collective-permute-done.3.b
  31.8 1.0 %collective-permute-done.4.c = f32[64,128]{1,0:T(8,128)S(1)} collective-permute-done((f32[64,128]{1,0:T(8,128)S(1)}, f32[64,128]{1,0:T(8,128)S(1)}, u32[]{:S(2)}, u32[]{:S(2)}) %collective-permute-start.4) | collective-permute-done | bytes 32800 | tf_op jit(solution)/shard_map/ppermute | solution.py:160
  32.9 1.3 %collective-permute-done.5.d = f32[64,128]{1,0:T(8,128)S(1)} collective-permute-done((f32[64,128]{1,0:T(8,128)S(1)}, f32[64,128]{1,0:T(8,128)S(1)}, u32[]{:S(2)}, u32[]{:S(2)}) %collective-permute-start.5) | collective-permute-done | bytes 32800 | tf_op jit(solution)/shard_map/ppermute | solution.py:160
  34.2 0.0 copy-done
  34.2 0.0 copy-done.1
  34.2 0.6 %update.1 = (f32[64,128]{1,0:T(8,128)}, f32[64,128]{1,0:T(8,128)}) custom-call(f32[64,128]{1,0:T(8,128)S(1)} %copy-done, f32[64,128]{1,0:T(8,128)S(1)} %copy-done.1, f32[64,128]{1,0:T(8,128)S(1)} %get-tuple-element.13.a, f32[64,128]{1,0:T(8,128)S(1)} %collective-permute-done.3.b, f32[64,128]{1,0:T(8,128)S(1)} %collective-permute-done.4.c, ...), custom_call_target="tpu_custom_call" | custom-call | tf_op jit(solution)/shard_map/update/pallas_call | solution.py:141
Async XLA Ops:
  0.6 14.1 %copy-start.2 = (s32[64]{0:T(128)S(1)}, s32[64]{0:T(128)}, u32[]{:S(2)}) copy-start(s32[64]{0:T(128)} %param.9) | copy-start | bytes 772
  3.3 23.8 %all-to-all-start = ((f32[32,33,1,128]{3,2,1,0:T(1,128)}), f32[32,33,1,128]{3,2,1,0:T(1,128)S(1)}, u32[]{:S(2)}, u32[]{:S(2)}) async-start(f32[32,33,1,128]{3,2,1,0:T(1,128)} %bitcast.19), calls=%async_computation | async-start | bytes 1081344 | tf_op jit(solution)/shard_map/all_to_all | solution.py:154
  14.7 12.5 %collective-permute-start.2 = (s32[1,64]{1,0:T(1,128)S(1)}, s32[1,64]{1,0:T(1,128)S(1)}, u32[]{:S(2)}, u32[]{:S(2)}) collective-permute-start(s32[1,64]{1,0:T(1,128)S(1)} %bitcast.10), channel_id=1, source_target_pairs={{0,3},{1,2},{2,1},{3,0},{4,7},{5,6},{6,5},{7,4},{8,11},{9,10},{10,... | collective-permute-start | bytes 776 | tf_op jit(solution)/shard_map/ppermute | solution.py:156
  16.0 11.1 %collective-permute-start.1 = (s32[1,64]{1,0:T(1,128)S(1)}, s32[1,64]{1,0:T(1,128)S(1)}, u32[]{:S(2)}, u32[]{:S(2)}) collective-permute-start(s32[1,64]{1,0:T(1,128)S(1)} %bitcast.11), channel_id=1, source_target_pairs={{0,2},{1,3},{2,0},{3,1},{4,6},{5,7},{6,4},{7,5},{8,10},{9,11},{10,... | collective-permute-start | bytes 776 | tf_op jit(solution)/shard_map/ppermute | solution.py:156
  17.1 10.1 %collective-permute-start = (s32[1,64]{1,0:T(1,128)S(1)}, s32[1,64]{1,0:T(1,128)S(1)}, u32[]{:S(2)}, u32[]{:S(2)}) collective-permute-start(s32[1,64]{1,0:T(1,128)S(1)} %bitcast.12), channel_id=1, source_target_pairs={{0,1},{1,0},{2,3},{3,2},{4,5},{5,4},{6,7},{7,6},{8,9},{9,8},{10,11... | collective-permute-start | bytes 776 | tf_op jit(solution)/shard_map/ppermute | solution.py:156
  17.1 17.1 %copy-start = (f32[64,128]{1,0:T(8,128)S(1)}, f32[64,128]{1,0:T(8,128)}, u32[]{:S(2)}) copy-start(f32[64,128]{1,0:T(8,128)} %momentum.1) | copy-start | bytes 98308
  17.1 17.1 %copy-start.1 = (f32[64,128]{1,0:T(8,128)S(1)}, f32[64,128]{1,0:T(8,128)}, u32[]{:S(2)}) copy-start(f32[64,128]{1,0:T(8,128)} %params.1) | copy-start | bytes 98308
  27.8 4.0 %collective-permute-start.3 = (f32[64,128]{1,0:T(8,128)S(1)}, f32[64,128]{1,0:T(8,128)S(1)}, u32[]{:S(2)}, u32[]{:S(2)}) collective-permute-start(f32[64,128]{1,0:T(8,128)S(1)} %get-tuple-element.14), channel_id=1, source_target_pairs={{0,1},{1,0},{2,3},{3,2},{4,5},{5,4},{6,7},{7,6},{8,9},{9,8},{10,11... | collective-permute-start | bytes 98312 | tf_op jit(solution)/shard_map/ppermute | solution.py:160
  30.1 2.8 %collective-permute-start.4 = (f32[64,128]{1,0:T(8,128)S(1)}, f32[64,128]{1,0:T(8,128)S(1)}, u32[]{:S(2)}, u32[]{:S(2)}) collective-permute-start(f32[64,128]{1,0:T(8,128)S(1)} %get-tuple-element.15), channel_id=1, source_target_pairs={{0,2},{1,3},{2,0},{3,1},{4,6},{5,7},{6,4},{7,5},{8,10},{9,11},{10,... | collective-permute-start | bytes 98312 | tf_op jit(solution)/shard_map/ppermute | solution.py:160
  30.5 3.7 %collective-permute-start.5 = (f32[64,128]{1,0:T(8,128)S(1)}, f32[64,128]{1,0:T(8,128)S(1)}, u32[]{:S(2)}, u32[]{:S(2)}) collective-permute-start(f32[64,128]{1,0:T(8,128)S(1)} %get-tuple-element.16), channel_id=1, source_target_pairs={{0,3},{1,2},{2,1},{3,0},{4,7},{5,6},{6,5},{7,4},{8,11},{9,10},{10,... | collective-permute-start | bytes 98312 | tf_op jit(solution)/shard_map/ppermute | solution.py:160

commit v2 on v1

v2 whole, which is shorter than its diff:
```python
import jax
import jax.numpy as jnp
from jax import lax
from jax.experimental import pallas as pl
from jax.experimental.pallas import tpu as pltpu
from jax.sharding import Mesh
from jax.sharding import PartitionSpec as P

DP = ("x", "z", "y", "c")
GATHER = ("x", "z")
SERVE = "y"
PEERS = 16
LANES = 128
STEP = 1024
CHUNKS = 8
EARLY = 5


def xor_pairs(bits):
    return [(i, i ^ bits) for i in range(4)]


def early_chunks():
    far = lax.axis_index("x") + lax.axis_index("z") + lax.axis_index("y")
    return jnp.clip(EARLY - far, 0, CHUNKS)


def chunk_loads(i, grads, error, gbuf, ebuf, gsem, esem):
    rows = pl.ds(i * STEP, STEP)
    return (
        pltpu.make_async_copy(grads.at[rows], gbuf.at[rows], gsem.at[i]),
        pltpu.make_async_copy(error.at[rows], ebuf.at[rows], esem.at[i]),
    )


def chunk_store(i, obuf, out, osem):
    rows = pl.ds(i * STEP, STEP)
    return pltpu.make_async_copy(obuf.at[i, pl.ds(0, STEP)], out.at[rows], osem.at[i])


def chunk_work(i, picks, gbuf, ebuf, obuf):
    rows = pl.ds(i * STEP, STEP)
    obuf[i, pl.ds(0, STEP), :] = gbuf[rows, :] + ebuf[rows, :]
    for k in range(picks.shape[0]):
        row = picks[k] - i * STEP
        row = jnp.where((row >= 0) & (row < STEP), row, STEP)
        obuf[i, pl.ds(row, 1), :] = jnp.zeros((1, LANES), jnp.float32)


def dense_chunks(wanted, picks, grads, error, out, gbuf, ebuf, obuf, gsem, esem, osem, first):
    for i in range(CHUNKS):

        @pl.when(wanted(i))
        def _():
            for copy in chunk_loads(i, grads, error, gbuf, ebuf, gsem, esem):
                copy.start()

    first()
    for i in range(CHUNKS):

        @pl.when(wanted(i))
        def _():
            for copy in chunk_loads(i, grads, error, gbuf, ebuf, gsem, esem):
                copy.wait()
            chunk_work(i, picks, gbuf, ebuf, obuf)
            chunk_store(i, obuf, out, osem).start()

    for i in range(CHUNKS):

        @pl.when(wanted(i))
        def _():
            chunk_store(i, obuf, out, osem).wait()


def dense_scratch(blocks):
    return [
        pltpu.VMEM((blocks, LANES), jnp.float32),
        pltpu.VMEM((blocks, LANES), jnp.float32),
        pltpu.VMEM((CHUNKS, STEP + 8, LANES), jnp.float32),
        pltpu.SemaphoreType.DMA((CHUNKS,)),
        pltpu.SemaphoreType.DMA((CHUNKS,)),
        pltpu.SemaphoreType.DMA((CHUNKS,)),
    ]


def rows_kernel(
    picks_hbm, grads, error, grads_rows, error_rows, send, out,
    picks, grow, erow, psem, rsem, ssem, gbuf, ebuf, obuf, gsem, esem, osem,
):
    fetch = pltpu.make_async_copy(picks_hbm, picks, psem)
    fetch.start()
    fetch.wait()
    count = picks.shape[0]
    for k in range(count):
        row = picks[k]
        pltpu.make_async_copy(grads_rows.at[pl.ds(row, 1)], grow.at[pl.ds(k, 1)], rsem).start()
        pltpu.make_async_copy(error_rows.at[pl.ds(row, 1)], erow.at[pl.ds(k, 1)], ssem).start()
    limit = early_chunks()

    def build():
        lane = lax.broadcasted_iota(jnp.int32, (1, LANES), 1) % count
        ids = jnp.zeros((1, LANES), jnp.int32)
        for k in range(count):
            ids = jnp.where(lane == k, picks[k], ids)
        pltpu.make_async_copy(grads_rows.at[pl.ds(0, count)], grow, rsem).wait()
        pltpu.make_async_copy(error_rows.at[pl.ds(0, count)], erow, ssem).wait()
        acc = grow[:, 0, :] + erow[:, 0, :]
        ids = ids.astype(jnp.float32)
        for p in range(PEERS):
            base = p * (count + 1)
            send[base : base + count, :] = acc
            send[base + count : base + count + 1, :] = ids

    dense_chunks(
        lambda i: i < limit, picks, grads, error, out, gbuf, ebuf, obuf, gsem, esem, osem, build
    )


def chosen_rows(picks, grads, error):
    count = picks.shape[0]
    return pl.pallas_call(
        rows_kernel,
        in_specs=[pl.BlockSpec(memory_space=pltpu.HBM)] * 5,
        out_specs=[pl.BlockSpec(memory_space=pltpu.VMEM), pl.BlockSpec(memory_space=pltpu.HBM)],
        scratch_shapes=[
            pltpu.SMEM((count,), jnp.int32),
            pltpu.VMEM((count, 1, LANES), jnp.float32),
            pltpu.VMEM((count, 1, LANES), jnp.float32),
            pltpu.SemaphoreType.DMA,
            pltpu.SemaphoreType.DMA,
            pltpu.SemaphoreType.DMA,
        ]
        + dense_scratch(grads.shape[0]),
        out_shape=[
            jax.ShapeDtypeStruct((PEERS * (count + 1), LANES), jnp.float32),
            jax.ShapeDtypeStruct(grads.shape, jnp.float32),
        ],
        name="chosen_rows",
    )(picks, grads, error, grads.reshape(-1, 1, LANES), error.reshape(-1, 1, LANES))


def late_kernel(
    picks_hbm, grads, error, begun, out,
    picks, psem, gbuf, ebuf, obuf, gsem, esem, osem,
):
    limit = early_chunks()

    @pl.when(limit < CHUNKS)
    def _():
        fetch = pltpu.make_async_copy(picks_hbm, picks, psem)
        fetch.start()
        dense_chunks(
            lambda i: i >= limit,
            picks, grads, error, out, gbuf, ebuf, obuf, gsem, esem, osem, fetch.wait,
        )


def remainder(picks, grads, error, begun):
    return pl.pallas_call(
        late_kernel,
        in_specs=[pl.BlockSpec(memory_space=pltpu.HBM)] * 4,
        out_specs=pl.BlockSpec(memory_space=pltpu.HBM),
        out_shape=jax.ShapeDtypeStruct(grads.shape, jnp.float32),
        input_output_aliases={3: 0},
        scratch_shapes=[pltpu.SMEM(picks.shape, jnp.int32), pltpu.SemaphoreType.DMA]
        + dense_scratch(grads.shape[0]),
        cost_estimate=pl.CostEstimate(
            flops=40_000_000, bytes_accessed=12 << 20, transcendentals=0
        ),
        name="remainder",
    )(picks, grads, error, begun)


def totals_kernel(mine, other, id0, id1, id2, id3, out0, out1, out2, out3):
    count = mine.shape[0] // PEERS - 1
    per = LANES // count
    lane = lax.broadcasted_iota(jnp.int32, (1, LANES), 1)
    slots = id0.shape[1]
    columns = []
    for ids in (id0, id1, id2, id3):
        wide = jnp.broadcast_to(ids[...].astype(jnp.float32), (LANES, slots))
        columns.append(wide.T)
    owned = jnp.concatenate(columns, axis=0)
    marks, values = [], []
    for g in range(2 * PEERS // per):
        ids = None
        got = mine if g < PEERS // per else other
        for q in range(per):
            base = (g * per + q) % PEERS * (count + 1)
            row = got[base + count : base + count + 1, :]
            ids = row if ids is None else jnp.where(lane < q * count, ids, row)
            values.append(got[base : base + count, :])
        marks.append(jnp.where(owned == ids, 1.0, 0.0).astype(jnp.bfloat16))
    marks = jnp.concatenate(marks, axis=1)
    values = jnp.concatenate(values, axis=0)
    total = None
    for _ in range(3):
        part = values.astype(jnp.bfloat16)
        values = values - part.astype(jnp.float32)
        term = jnp.dot(marks, part, preferred_element_type=jnp.float32)
        total = term if total is None else total + term
    for j, out in enumerate((out0, out1, out2, out3)):
        out[...] = total[j * slots : (j + 1) * slots, :]


def totals(mine, other, ids):
    slots = ids[0].shape[1]
    return pl.pallas_call(
        totals_kernel,
        out_shape=[jax.ShapeDtypeStruct((slots, LANES), jnp.float32)] * 4,
        compiler_params=pltpu.CompilerParams(vmem_limit_bytes=8 << 20),
        name="totals",
    )(mine, other, *ids)


def update_kernel(momentum, params, a, b, c, d, new_params, new_momentum):
    fresh = 0.9 * momentum[...] + ((a[...] + b[...]) + (c[...] + d[...]))
    new_momentum[...] = fresh
    new_params[...] = params[...] - 0.5 * fresh


def update(momentum, params, parts):
    shape = jax.ShapeDtypeStruct(params.shape, jnp.float32)
    return pl.pallas_call(
        update_kernel,
        out_shape=[shape, shape],
        compiler_params=pltpu.CompilerParams(vmem_limit_bytes=2 << 20),
        name="update",
    )(momentum, params, *parts)


def swapped(x, bits):
    return lax.ppermute(x, SERVE, xor_pairs(bits))


def on_device(grads, error, picks, owned_ids, params, momentum):
    return step(grads[0], error[0], picks[0], owned_ids, params, momentum)


def step(grads, error, picks, owned_ids, params, momentum):
    count = picks.shape[0]
    send, begun = chosen_rows(picks, grads, error)
    send = send.reshape(PEERS, count + 1, 1, LANES)
    got = lax.all_to_all(send, GATHER, 0, 0, tiled=True)
    mine = owned_ids.reshape(1, -1)
    ids = [mine] + [swapped(mine, b) for b in (1, 2, 3)]
    got = got.reshape(-1, LANES)
    other = lax.ppermute(got, "c", [(0, 1), (1, 0)])
    parts = totals(got, other, ids)
    new_error = remainder(picks, grads, error, begun)
    parts = [parts[0]] + [swapped(parts[b], b) for b in (1, 2, 3)]
    new_params, new_momentum = update(momentum, params, parts)
    return new_error[None], new_params, new_momentum


def solution(mesh):
    split = Mesh(mesh.devices.reshape(4, 4, 4, 2), DP)
    return jax.shard_map(
        on_device,
        mesh=split,
        in_specs=(
            P(DP, None, None),
            P(DP, None, None),
            P(DP, None),
            P(DP),
            P(DP, None),
            P(DP, None),
        ),
        out_specs=(P(DP, None, None), P(DP, None), P(DP, None)),
        check_vma=False,
    )
```

time: 35.3 us -> 38.7 us (1.096)
  the two profiles are of different devices: /device:TPU:1 before, /device:TPU:0 now
where the time goes in v2:
time: 38.7 us; the launch traced here: 38.5 us
  blocking collectives  14.6 us (38%)
  Pallas kernels  10 us (26%)
  starting transfers between devices  9.47 us (24%)
  waiting for transfers between devices  3.71 us (10%)
  between operations  0.69 us (2%)
    all_to_all x1, blocking collectives, step(): got = lax.all_to_all(send, GATHER, 0, 0, tiled=True)  14.6 us
    ppermute x6, starting transfers between devices, swapped(): return lax.ppermute(x, SERVE, xor_pairs(bits))  9.47 us
    pallas_call x1, Pallas kernels, chosen_rows(): pl.pallas_call(rows_kernel, in_specs=[pl.BlockSpec(memory_space=pltpu.HBM...  5.79 us
    ppermute x6, waiting for transfers between devices, swapped(): return lax.ppermute(x, SERVE, xor_pairs(bits))  3.71 us
    pallas_call x1, Pallas kernels, remainder(): pl.pallas_call(late_kernel, in_specs=[pl.BlockSpec(memory_space=pltpu.HBM...  2.94 us
  transfers between devices with their start and end apart: 7, of which 3 were waited for; matrix products, arithmetic and copies ran while one was open for 0% of the time, Pallas kernels for 8%

profile of v2, /device:TPU:0, one launch (start us, length us, event | category | flops | bytes accessed | tf_op | source)
XLA Modules:
  0.0 38.5 jit_solution(6295348800962038116)
XLA Ops:
  0.6 0.0 copy-start.2
  0.6 5.8 %chosen_rows.1 = (f32[528,128]{1,0:T(8,128)}, f32[8192,128]{1,0:T(8,128)}) custom-call(s32[32]{0:T(128)} %bitcast.23, f32[8192,128]{1,0:T(8,128)} %bitcast.15, f32[8192,128]{1,0:T(8,128)} %bitcast.18, f32[8192,1,128]{2,1,0:T(1,128)} %bitcast.16, f32[8192,1,128]{2,1,0:T(1,128)} %bitcast.19), custom_call_target="tpu_custom_call" | custom-call | tf_op jit(solution)/shard_map/chosen_rows/pallas_call | solution.py:121
  6.4 14.6 %all_to_all.5 = f32[16,33,1,128]{3,2,1,0:T(1,128)S(1)} all-to-all(f32[16,33,1,128]{3,2,1,0:T(1,128)} %bitcast.22), channel_id=1, replica_groups=mesh['x'=4,'z'=4,'y'=4,'c'=2] {'x','z'}, dimensions={0} | all-to-all | bytes 540672 | tf_op jit(solution)/shard_map/all_to_all | solution.py:244
  21.1 0.0 collective-permute-start
  21.1 0.0 copy-done.2
  21.1 0.5 %collective-permute-start.1 = (s32[1,64]{1,0:T(1,128)S(1)}, s32[1,64]{1,0:T(1,128)S(1)}, u32[]{:S(2)}, u32[]{:S(2)}) collective-permute-start(s32[1,64]{1,0:T(1,128)S(1)} %bitcast.11), channel_id=1, source_target_pairs={{0,2},{2,0},{4,6},{6,4},{1,3},{3,1},{5,7},{7,5},{8,10},{10,8},{12,... | collective-permute-start | bytes 776 | tf_op jit(solution)/shard_map/ppermute | solution.py:233
  21.5 2.9 %collective-permute-start.2 = (s32[1,64]{1,0:T(1,128)S(1)}, s32[1,64]{1,0:T(1,128)S(1)}, u32[]{:S(2)}, u32[]{:S(2)}) collective-permute-start(s32[1,64]{1,0:T(1,128)S(1)} %bitcast.12), channel_id=1, source_target_pairs={{0,4},{2,6},{4,0},{6,2},{1,5},{3,7},{5,1},{7,3},{8,12},{10,14},{12... | collective-permute-start | bytes 776 | tf_op jit(solution)/shard_map/ppermute | solution.py:233
  24.4 1.3 %collective-permute-start.3 = (s32[1,64]{1,0:T(1,128)S(1)}, s32[1,64]{1,0:T(1,128)S(1)}, u32[]{:S(2)}, u32[]{:S(2)}) collective-permute-start(s32[1,64]{1,0:T(1,128)S(1)} %bitcast.13), channel_id=1, source_target_pairs={{0,6},{2,4},{4,2},{6,0},{1,7},{3,5},{5,3},{7,1},{8,14},{10,12},{12... | collective-permute-start | bytes 776 | tf_op jit(solution)/shard_map/ppermute | solution.py:233
  25.8 0.0 collective-permute-done.1.id1
  25.8 0.8 %collective-permute-done.2.id2 = s32[1,64]{1,0:T(1,128)S(1)} collective-permute-done((s32[1,64]{1,0:T(1,128)S(1)}, s32[1,64]{1,0:T(1,128)S(1)}, u32[]{:S(2)}, u32[]{:S(2)}) %collective-permute-start.2) | collective-permute-done | bytes 288 | tf_op jit(solution)/shard_map/ppermute | solution.py:233
  26.6 2.6 %collective-permute-done.3.id3 = s32[1,64]{1,0:T(1,128)S(1)} collective-permute-done((s32[1,64]{1,0:T(1,128)S(1)}, s32[1,64]{1,0:T(1,128)S(1)}, u32[]{:S(2)}, u32[]{:S(2)}) %collective-permute-start.3) | collective-permute-done | bytes 288 | tf_op jit(solution)/shard_map/ppermute | solution.py:233
  29.2 0.0 collective-permute-done.other
  29.2 0.6 %totals.1 = (f32[64,128]{1,0:T(8,128)S(1)}, f32[64,128]{1,0:T(8,128)S(1)}, f32[64,128]{1,0:T(8,128)S(1)}, f32[64,128]{1,0:T(8,128)S(1)}) custom-call(f32[528,128]{1,0:T(8,128)S(1)} %bitcast.10, f32[528,128]{1,0:T(8,128)S(1)} %collective-permute-done.other, s32[1,64]{1,0:T(1,128)S(1)} %bitcast.14, s32[1,64]{1,0:T(1,128)S(1)} %collective-permute-done.1.id1, ...), custom_call_target="tpu_custom_call" | custom-call | tf_op jit(solution)/shard_map/totals/pallas_call | solution.py:208
  29.9 0.1 collective-permute-start.4
  30.0 2.8 %collective-permute-start.5 = (f32[64,128]{1,0:T(8,128)S(1)}, f32[64,128]{1,0:T(8,128)S(1)}, u32[]{:S(2)}, u32[]{:S(2)}) collective-permute-start(f32[64,128]{1,0:T(8,128)S(1)} %get-tuple-element.15), channel_id=1, source_target_pairs={{0,4},{2,6},{4,0},{6,2},{1,5},{3,7},{5,1},{7,3},{8,12},{10,14},{12... | collective-permute-start | bytes 98312 | tf_op jit(solution)/shard_map/ppermute | solution.py:233
  32.7 1.9 %collective-permute-start.6 = (f32[64,128]{1,0:T(8,128)S(1)}, f32[64,128]{1,0:T(8,128)S(1)}, u32[]{:S(2)}, u32[]{:S(2)}) collective-permute-start(f32[64,128]{1,0:T(8,128)S(1)} %get-tuple-element.16), channel_id=1, source_target_pairs={{0,6},{2,4},{4,2},{6,0},{1,7},{3,5},{5,3},{7,1},{8,14},{10,12},{12... | collective-permute-start | bytes 98312 | tf_op jit(solution)/shard_map/ppermute | solution.py:233
  34.6 0.0 copy-start
  34.6 0.0 copy-start.1
  34.6 2.9 %remainder.1 = f32[8192,128]{1,0:T(8,128)} custom-call(s32[32]{0:T(128)} %bitcast.24, f32[8192,128]{1,0:T(8,128)} %bitcast.17, f32[8192,128]{1,0:T(8,128)} %bitcast.20, f32[8192,128]{1,0:T(8,128)} %get-tuple-element.11.begun), custom_call_target="tpu_custom_call", output_to_operand_aliasing={{}: (3, {})} | custom-call | flops 40000000 | bytes 12582912 | tf_op jit(solution)/shard_map/remainder/pallas_call | solution.py:159
  37.6 0.0 collective-permute-done.4.b
  37.6 0.0 collective-permute-done.5.c
  37.6 0.2 collective-permute-done.6.d
  37.9 0.0 copy-done
  37.9 0.0 copy-done.1
  37.9 0.6 %update.1 = (f32[64,128]{1,0:T(8,128)}, f32[64,128]{1,0:T(8,128)}) custom-call(f32[64,128]{1,0:T(8,128)S(1)} %copy-done, f32[64,128]{1,0:T(8,128)S(1)} %copy-done.1, f32[64,128]{1,0:T(8,128)S(1)} %get-tuple-element.13.a, f32[64,128]{1,0:T(8,128)S(1)} %collective-permute-done.4.b, f32[64,128]{1,0:T(8,128)S(1)} %collective-permute-done.5.c, ...), custom_call_target="tpu_custom_call" | custom-call | tf_op jit(solution)/shard_map/update/pallas_call | solution.py:224
Async XLA Ops:
  0.6 20.4 %copy-start.2 = (s32[64]{0:T(128)S(1)}, s32[64]{0:T(128)}, u32[]{:S(2)}) copy-start(s32[64]{0:T(128)} %param.9) | copy-start | bytes 772
  21.1 8.2 %collective-permute-start = (f32[528,128]{1,0:T(8,128)S(1)}, f32[528,128]{1,0:T(8,128)S(1)}, u32[]{:S(2)}, u32[]{:S(2)}) collective-permute-start(f32[528,128]{1,0:T(8,128)S(1)} %bitcast.9), channel_id=1, source_target_pairs={{0,1},{1,0},{2,3},{3,2},{4,5},{5,4},{6,7},{7,6},{8,9},{9,8},{10,11... | collective-permute-start | bytes 811016 | tf_op jit(solution)/shard_map/ppermute | solution.py:248
  21.1 4.7 %collective-permute-start.1 = (s32[1,64]{1,0:T(1,128)S(1)}, s32[1,64]{1,0:T(1,128)S(1)}, u32[]{:S(2)}, u32[]{:S(2)}) collective-permute-start(s32[1,64]{1,0:T(1,128)S(1)} %bitcast.11), channel_id=1, source_target_pairs={{0,2},{2,0},{4,6},{6,4},{1,3},{3,1},{5,7},{7,5},{8,10},{10,8},{12,... | collective-permute-start | bytes 776 | tf_op jit(solution)/shard_map/ppermute | solution.py:233
  21.5 5.1 %collective-permute-start.2 = (s32[1,64]{1,0:T(1,128)S(1)}, s32[1,64]{1,0:T(1,128)S(1)}, u32[]{:S(2)}, u32[]{:S(2)}) collective-permute-start(s32[1,64]{1,0:T(1,128)S(1)} %bitcast.12), channel_id=1, source_target_pairs={{0,4},{2,6},{4,0},{6,2},{1,5},{3,7},{5,1},{7,3},{8,12},{10,14},{12... | collective-permute-start | bytes 776 | tf_op jit(solution)/shard_map/ppermute | solution.py:233
  24.4 4.8 %collective-permute-start.3 = (s32[1,64]{1,0:T(1,128)S(1)}, s32[1,64]{1,0:T(1,128)S(1)}, u32[]{:S(2)}, u32[]{:S(2)}) collective-permute-start(s32[1,64]{1,0:T(1,128)S(1)} %bitcast.13), channel_id=1, source_target_pairs={{0,6},{2,4},{4,2},{6,0},{1,7},{3,5},{5,3},{7,1},{8,14},{10,12},{12... | collective-permute-start | bytes 776 | tf_op jit(solution)/shard_map/ppermute | solution.py:233
  29.9 7.7 %collective-permute-start.4 = (f32[64,128]{1,0:T(8,128)S(1)}, f32[64,128]{1,0:T(8,128)S(1)}, u32[]{:S(2)}, u32[]{:S(2)}) collective-permute-start(f32[64,128]{1,0:T(8,128)S(1)} %get-tuple-element.14), channel_id=1, source_target_pairs={{0,2},{2,0},{4,6},{6,4},{1,3},{3,1},{5,7},{7,5},{8,10},{10,8},{12,... | collective-permute-start | bytes 98312 | tf_op jit(solution)/shard_map/ppermute | solution.py:233
  30.0 7.6 %collective-permute-start.5 = (f32[64,128]{1,0:T(8,128)S(1)}, f32[64,128]{1,0:T(8,128)S(1)}, u32[]{:S(2)}, u32[]{:S(2)}) collective-permute-start(f32[64,128]{1,0:T(8,128)S(1)} %get-tuple-element.15), channel_id=1, source_target_pairs={{0,4},{2,6},{4,0},{6,2},{1,5},{3,7},{5,1},{7,3},{8,12},{10,14},{12... | collective-permute-start | bytes 98312 | tf_op jit(solution)/shard_map/ppermute | solution.py:233
  32.7 5.1 %collective-permute-start.6 = (f32[64,128]{1,0:T(8,128)S(1)}, f32[64,128]{1,0:T(8,128)S(1)}, u32[]{:S(2)}, u32[]{:S(2)}) collective-permute-start(f32[64,128]{1,0:T(8,128)S(1)} %get-tuple-element.16), channel_id=1, source_target_pairs={{0,6},{2,4},{4,2},{6,0},{1,7},{3,5},{5,3},{7,1},{8,14},{10,12},{12... | collective-permute-start | bytes 98312 | tf_op jit(solution)/shard_map/ppermute | solution.py:233
  34.6 3.2 %copy-start = (f32[64,128]{1,0:T(8,128)S(1)}, f32[64,128]{1,0:T(8,128)}, u32[]{:S(2)}) copy-start(f32[64,128]{1,0:T(8,128)} %momentum.1) | copy-start | bytes 98308
  34.6 3.2 %copy-start.1 = (f32[64,128]{1,0:T(8,128)S(1)}, f32[64,128]{1,0:T(8,128)}, u32[]{:S(2)}) copy-start(f32[64,128]{1,0:T(8,128)} %params.1) | copy-start | bytes 98308

commit v3 on v2

--- a/solution.py
+++ b/solution.py
@@ -3,12 +3,9 @@
 from jax import lax
 from jax.experimental import pallas as pl
 from jax.experimental.pallas import tpu as pltpu
-from jax.sharding import Mesh
 from jax.sharding import PartitionSpec as P
 
-DP = ("x", "z", "y", "c")
-GATHER = ("x", "z")
-SERVE = "y"
+DP = "dp"
 PEERS = 16
 LANES = 128
 STEP = 1024
@@ -16,12 +13,24 @@
 EARLY = 5
 
 
-def xor_pairs(bits):
-    return [(i, i ^ bits) for i in range(4)]
+def rank(x, z, y, c):
+    return ((x * 4 + z) * 4 + y) * 2 + c
+
+
+def partners(zbits, cbits):
+    ranks = range(128)
+    return [(i, i ^ (zbits * 8) ^ cbits) for i in ranks]
+
+
+def planes():
+    order = [(x, y) for x in range(4) for y in range(4)]
+    order = sorted(order, key=lambda p: (p != (2, 2), -p[0], -p[1]))
+    return [[rank(x, z, y, c) for x, y in order] for z in range(4) for c in range(2)]
 
 
 def early_chunks():
-    far = lax.axis_index("x") + lax.axis_index("z") + lax.axis_index("y")
+    here = lax.axis_index(DP)
+    far = here // 32 + here // 8 % 4 + here // 2 % 4
     return jnp.clip(EARLY - far, 0, CHUNKS)
 
 
@@ -230,7 +239,7 @@
 
 
 def swapped(x, bits):
-    return lax.ppermute(x, SERVE, xor_pairs(bits))
+    return lax.ppermute(x, DP, partners(bits, 0))
 
 
 def on_device(grads, error, picks, owned_ids, params, momentum):
@@ -241,11 +250,11 @@
     count = picks.shape[0]
     send, begun = chosen_rows(picks, grads, error)
     send = send.reshape(PEERS, count + 1, 1, LANES)
-    got = lax.all_to_all(send, GATHER, 0, 0, tiled=True)
+    got = lax.all_to_all(send, DP, 0, 0, tiled=True, axis_index_groups=planes())
     mine = owned_ids.reshape(1, -1)
     ids = [mine] + [swapped(mine, b) for b in (1, 2, 3)]
     got = got.reshape(-1, LANES)
-    other = lax.ppermute(got, "c", [(0, 1), (1, 0)])
+    other = lax.ppermute(got, DP, partners(0, 1))
     parts = totals(got, other, ids)
     new_error = remainder(picks, grads, error, begun)
     parts = [parts[0]] + [swapped(parts[b], b) for b in (1, 2, 3)]
@@ -254,10 +263,9 @@
 
 
 def solution(mesh):
-    split = Mesh(mesh.devices.reshape(4, 4, 4, 2), DP)
     return jax.shard_map(
         on_device,
-        mesh=split,
+        mesh=mesh,
         in_specs=(
             P(DP, None, None),
             P(DP, None, None),

time: 38.7 us -> 37.8 us (0.977)
  the two profiles are of different devices: /device:TPU:0 before, /device:TPU:30 now
where the time goes in v3:
time: 37.8 us; the launch traced here: 37.6 us
  blocking collectives  13.6 us (36%)
  starting transfers between devices  9.47 us (25%)
  Pallas kernels  9.43 us (25%)
  waiting for transfers between devices  4.33 us (11%)
  between operations  0.71 us (2%)
    all_to_all x1, blocking collectives, step(): got = lax.all_to_all(send, DP, 0, 0, tiled=True, axis_index_groups=planes())  13.6 us
    ppermute x6, starting transfers between devices, swapped(): return lax.ppermute(x, DP, partners(bits, 0))  9.47 us
    pallas_call x1, Pallas kernels, remainder(): pl.pallas_call(late_kernel, in_specs=[pl.BlockSpec(memory_space=pltpu.HBM...  5.42 us
    ppermute x6, waiting for transfers between devices, swapped(): return lax.ppermute(x, DP, partners(bits, 0))  4.33 us
    pallas_call x1, Pallas kernels, chosen_rows(): pl.pallas_call(rows_kernel, in_specs=[pl.BlockSpec(memory_space=pltpu.HBM...  2.72 us
  transfers between devices with their start and end apart: 7, of which 2 were waited for; matrix products, arithmetic and copies ran while one was open for 0% of the time, Pallas kernels for 14%

profile of v3, /device:TPU:30, one launch (start us, length us, event | category | flops | bytes accessed | tf_op | source)
XLA Modules:
  0.0 37.6 jit_solution(11092245812388860585)
XLA Ops:
  0.6 0.0 copy-start.2
  0.6 2.7 %chosen_rows.1 = (f32[528,128]{1,0:T(8,128)}, f32[8192,128]{1,0:T(8,128)}) custom-call(s32[32]{0:T(128)} %bitcast.23, f32[8192,128]{1,0:T(8,128)} %bitcast.15, f32[8192,128]{1,0:T(8,128)} %bitcast.18, f32[8192,1,128]{2,1,0:T(1,128)} %bitcast.16, f32[8192,1,128]{2,1,0:T(1,128)} %bitcast.19), custom_call_target="tpu_custom_call" | custom-call | tf_op jit(solution)/shard_map/chosen_rows/pallas_call | solution.py:130
  3.4 13.6 %all_to_all.5 = f32[16,33,1,128]{3,2,1,0:T(1,128)S(1)} all-to-all(f32[16,33,1,128]{3,2,1,0:T(1,128)} %bitcast.22), channel_id=1, replica_groups={{68,102,100,98,96,70,66,64,38,36,34,32,6,4,2,0},{69,103,101,99,97,71,67..., dimensions={0} | all-to-all | bytes 540672 | tf_op jit(solution)/shard_map/all_to_all | solution.py:253
  17.0 0.0 collective-permute-start
  17.0 0.0 copy-done.2
  17.0 1.1 %collective-permute-start.1 = (s32[1,64]{1,0:T(1,128)S(1)}, s32[1,64]{1,0:T(1,128)S(1)}, u32[]{:S(2)}, u32[]{:S(2)}) collective-permute-start(s32[1,64]{1,0:T(1,128)S(1)} %bitcast.11), channel_id=1, source_target_pairs={{0,8},{1,9},{2,10},{3,11},{4,12},{5,13},{6,14},{7,15},{8,0},{9,1},... | collective-permute-start | bytes 776 | tf_op jit(solution)/shard_map/ppermute | solution.py:242
  18.1 3.1 %collective-permute-start.2 = (s32[1,64]{1,0:T(1,128)S(1)}, s32[1,64]{1,0:T(1,128)S(1)}, u32[]{:S(2)}, u32[]{:S(2)}) collective-permute-start(s32[1,64]{1,0:T(1,128)S(1)} %bitcast.12), channel_id=1, source_target_pairs={{0,16},{1,17},{2,18},{3,19},{4,20},{5,21},{6,22},{7,23},{8,24},{9,... | collective-permute-start | bytes 776 | tf_op jit(solution)/shard_map/ppermute | solution.py:242
  21.2 0.5 %collective-permute-start.3 = (s32[1,64]{1,0:T(1,128)S(1)}, s32[1,64]{1,0:T(1,128)S(1)}, u32[]{:S(2)}, u32[]{:S(2)}) collective-permute-start(s32[1,64]{1,0:T(1,128)S(1)} %bitcast.13), channel_id=1, source_target_pairs={{0,24},{1,25},{2,26},{3,27},{4,28},{5,29},{6,30},{7,31},{8,16},{9,... | collective-permute-start | bytes 776 | tf_op jit(solution)/shard_map/ppermute | solution.py:242
  21.7 0.0 collective-permute-done.1.id1
  21.7 1.5 %collective-permute-done.2.id2 = s32[1,64]{1,0:T(1,128)S(1)} collective-permute-done((s32[1,64]{1,0:T(1,128)S(1)}, s32[1,64]{1,0:T(1,128)S(1)}, u32[]{:S(2)}, u32[]{:S(2)}) %collective-permute-start.2) | collective-permute-done | bytes 288 | tf_op jit(solution)/shard_map/ppermute | solution.py:242
  23.2 2.8 %collective-permute-done.3.id3 = s32[1,64]{1,0:T(1,128)S(1)} collective-permute-done((s32[1,64]{1,0:T(1,128)S(1)}, s32[1,64]{1,0:T(1,128)S(1)}, u32[]{:S(2)}, u32[]{:S(2)}) %collective-permute-start.3) | collective-permute-done | bytes 288 | tf_op jit(solution)/shard_map/ppermute | solution.py:242
  26.0 0.0 collective-permute-done.other
  26.0 0.6 %totals.1 = (f32[64,128]{1,0:T(8,128)S(1)}, f32[64,128]{1,0:T(8,128)S(1)}, f32[64,128]{1,0:T(8,128)S(1)}, f32[64,128]{1,0:T(8,128)S(1)}) custom-call(f32[528,128]{1,0:T(8,128)S(1)} %bitcast.10, f32[528,128]{1,0:T(8,128)S(1)} %collective-permute-done.other, s32[1,64]{1,0:T(1,128)S(1)} %bitcast.14, s32[1,64]{1,0:T(1,128)S(1)} %collective-permute-done.1.id1, ...), custom_call_target="tpu_custom_call" | custom-call | tf_op jit(solution)/shard_map/totals/pallas_call | solution.py:217
  26.7 0.1 collective-permute-start.4
  26.7 1.9 %collective-permute-start.5 = (f32[64,128]{1,0:T(8,128)S(1)}, f32[64,128]{1,0:T(8,128)S(1)}, u32[]{:S(2)}, u32[]{:S(2)}) collective-permute-start(f32[64,128]{1,0:T(8,128)S(1)} %get-tuple-element.15), channel_id=1, source_target_pairs={{0,16},{1,17},{2,18},{3,19},{4,20},{5,21},{6,22},{7,23},{8,24},{9,... | collective-permute-start | bytes 98312 | tf_op jit(solution)/shard_map/ppermute | solution.py:242
  28.7 2.8 %collective-permute-start.6 = (f32[64,128]{1,0:T(8,128)S(1)}, f32[64,128]{1,0:T(8,128)S(1)}, u32[]{:S(2)}, u32[]{:S(2)}) collective-permute-start(f32[64,128]{1,0:T(8,128)S(1)} %get-tuple-element.16), channel_id=1, source_target_pairs={{0,24},{1,25},{2,26},{3,27},{4,28},{5,29},{6,30},{7,31},{8,16},{9,... | collective-permute-start | bytes 98312 | tf_op jit(solution)/shard_map/ppermute | solution.py:242
  31.4 0.0 copy-start
  31.4 0.0 copy-start.1
  31.4 5.4 %remainder.1 = f32[8192,128]{1,0:T(8,128)} custom-call(s32[32]{0:T(128)} %bitcast.24, f32[8192,128]{1,0:T(8,128)} %bitcast.17, f32[8192,128]{1,0:T(8,128)} %bitcast.20, f32[8192,128]{1,0:T(8,128)} %get-tuple-element.11.begun), custom_call_target="tpu_custom_call", output_to_operand_aliasing={{}: (3, {})} | custom-call | flops 40000000 | bytes 12582912 | tf_op jit(solution)/shard_map/remainder/pallas_call | solution.py:168
  36.9 0.0 collective-permute-done.4.b
  36.9 0.0 collective-permute-done.5.c
  36.9 0.0 collective-permute-done.6.d
  36.9 0.0 copy-done
  36.9 0.0 copy-done.1
  36.9 0.6 %update.1 = (f32[64,128]{1,0:T(8,128)}, f32[64,128]{1,0:T(8,128)}) custom-call(f32[64,128]{1,0:T(8,128)S(1)} %copy-done, f32[64,128]{1,0:T(8,128)S(1)} %copy-done.1, f32[64,128]{1,0:T(8,128)S(1)} %get-tuple-element.13.a, f32[64,128]{1,0:T(8,128)S(1)} %collective-permute-done.4.b, f32[64,128]{1,0:T(8,128)S(1)} %collective-permute-done.5.c, ...), custom_call_target="tpu_custom_call" | custom-call | tf_op jit(solution)/shard_map/update/pallas_call | solution.py:233
Async XLA Ops:
  0.6 16.3 %copy-start.2 = (s32[64]{0:T(128)S(1)}, s32[64]{0:T(128)}, u32[]{:S(2)}) copy-start(s32[64]{0:T(128)} %param.9) | copy-start | bytes 772
  17.0 9.0 %collective-permute-start = (f32[528,128]{1,0:T(8,128)S(1)}, f32[528,128]{1,0:T(8,128)S(1)}, u32[]{:S(2)}, u32[]{:S(2)}) collective-permute-start(f32[528,128]{1,0:T(8,128)S(1)} %bitcast.9), channel_id=1, source_target_pairs={{0,1},{1,0},{2,3},{3,2},{4,5},{5,4},{6,7},{7,6},{8,9},{9,8},{10,11... | collective-permute-start | bytes 811016 | tf_op jit(solution)/shard_map/ppermute | solution.py:257
  17.0 4.7 %collective-permute-start.1 = (s32[1,64]{1,0:T(1,128)S(1)}, s32[1,64]{1,0:T(1,128)S(1)}, u32[]{:S(2)}, u32[]{:S(2)}) collective-permute-start(s32[1,64]{1,0:T(1,128)S(1)} %bitcast.11), channel_id=1, source_target_pairs={{0,8},{1,9},{2,10},{3,11},{4,12},{5,13},{6,14},{7,15},{8,0},{9,1},... | collective-permute-start | bytes 776 | tf_op jit(solution)/shard_map/ppermute | solution.py:242
  18.1 5.1 %collective-permute-start.2 = (s32[1,64]{1,0:T(1,128)S(1)}, s32[1,64]{1,0:T(1,128)S(1)}, u32[]{:S(2)}, u32[]{:S(2)}) collective-permute-start(s32[1,64]{1,0:T(1,128)S(1)} %bitcast.12), channel_id=1, source_target_pairs={{0,16},{1,17},{2,18},{3,19},{4,20},{5,21},{6,22},{7,23},{8,24},{9,... | collective-permute-start | bytes 776 | tf_op jit(solution)/shard_map/ppermute | solution.py:242
  21.2 4.8 %collective-permute-start.3 = (s32[1,64]{1,0:T(1,128)S(1)}, s32[1,64]{1,0:T(1,128)S(1)}, u32[]{:S(2)}, u32[]{:S(2)}) collective-permute-start(s32[1,64]{1,0:T(1,128)S(1)} %bitcast.13), channel_id=1, source_target_pairs={{0,24},{1,25},{2,26},{3,27},{4,28},{5,29},{6,30},{7,31},{8,16},{9,... | collective-permute-start | bytes 776 | tf_op jit(solution)/shard_map/ppermute | solution.py:242
  26.7 10.2 %collective-permute-start.4 = (f32[64,128]{1,0:T(8,128)S(1)}, f32[64,128]{1,0:T(8,128)S(1)}, u32[]{:S(2)}, u32[]{:S(2)}) collective-permute-start(f32[64,128]{1,0:T(8,128)S(1)} %get-tuple-element.14), channel_id=1, source_target_pairs={{0,8},{1,9},{2,10},{3,11},{4,12},{5,13},{6,14},{7,15},{8,0},{9,1},... | collective-permute-start | bytes 98312 | tf_op jit(solution)/shard_map/ppermute | solution.py:242
  26.7 10.1 %collective-permute-start.5 = (f32[64,128]{1,0:T(8,128)S(1)}, f32[64,128]{1,0:T(8,128)S(1)}, u32[]{:S(2)}, u32[]{:S(2)}) collective-permute-start(f32[64,128]{1,0:T(8,128)S(1)} %get-tuple-element.15), channel_id=1, source_target_pairs={{0,16},{1,17},{2,18},{3,19},{4,20},{5,21},{6,22},{7,23},{8,24},{9,... | collective-permute-start | bytes 98312 | tf_op jit(solution)/shard_map/ppermute | solution.py:242
  28.7 8.2 %collective-permute-start.6 = (f32[64,128]{1,0:T(8,128)S(1)}, f32[64,128]{1,0:T(8,128)S(1)}, u32[]{:S(2)}, u32[]{:S(2)}) collective-permute-start(f32[64,128]{1,0:T(8,128)S(1)} %get-tuple-element.16), channel_id=1, source_target_pairs={{0,24},{1,25},{2,26},{3,27},{4,28},{5,29},{6,30},{7,31},{8,16},{9,... | collective-permute-start | bytes 98312 | tf_op jit(solution)/shard_map/ppermute | solution.py:242
  31.4 5.5 %copy-start = (f32[64,128]{1,0:T(8,128)S(1)}, f32[64,128]{1,0:T(8,128)}, u32[]{:S(2)}) copy-start(f32[64,128]{1,0:T(8,128)} %momentum.1) | copy-start | bytes 98308
  31.4 5.5 %copy-start.1 = (f32[64,128]{1,0:T(8,128)S(1)}, f32[64,128]{1,0:T(8,128)}, u32[]{:S(2)}) copy-start(f32[64,128]{1,0:T(8,128)} %params.1) | copy-start | bytes 98308

commit v4 on v3

--- a/solution.py
+++ b/solution.py
@@ -11,6 +11,7 @@
 STEP = 1024
 CHUNKS = 8
 EARLY = 5
+MEET = ((2, 2), (2, 2), (2, 2), (3, 3))
 
 
 def rank(x, z, y, c):
@@ -23,9 +24,12 @@
 
 
 def planes():
-    order = [(x, y) for x in range(4) for y in range(4)]
-    order = sorted(order, key=lambda p: (p != (2, 2), -p[0], -p[1]))
-    return [[rank(x, z, y, c) for x, y in order] for z in range(4) for c in range(2)]
+    cells = [(x, y) for x in range(4) for y in range(4)]
+    groups = []
+    for z in range(4):
+        order = sorted(cells, key=lambda p: (p != MEET[z], -p[0], -p[1]))
+        groups += [[rank(x, z, y, c) for x, y in order] for c in range(2)]
+    return groups
 
 
 def early_chunks():

time: 37.8 us -> 37.8 us (level)
  no operation moved by 1% of the time
where the time goes in v4:
time: 37.8 us; the launch traced here: 37.6 us
  blocking collectives  13.6 us (36%)
  starting transfers between devices  9.47 us (25%)
  Pallas kernels  9.42 us (25%)
  waiting for transfers between devices  4.37 us (12%)
  between operations  0.71 us (2%)
    all_to_all x1, blocking collectives, step(): got = lax.all_to_all(send, DP, 0, 0, tiled=True, axis_index_groups=planes())  13.6 us
    ppermute x6, starting transfers between devices, swapped(): return lax.ppermute(x, DP, partners(bits, 0))  9.47 us
    pallas_call x1, Pallas kernels, remainder(): pl.pallas_call(late_kernel, in_specs=[pl.BlockSpec(memory_space=pltpu.HBM...  5.42 us
    ppermute x6, waiting for transfers between devices, swapped(): return lax.ppermute(x, DP, partners(bits, 0))  4.37 us
    pallas_call x1, Pallas kernels, chosen_rows(): pl.pallas_call(rows_kernel, in_specs=[pl.BlockSpec(memory_space=pltpu.HBM...  2.72 us
  transfers between devices with their start and end apart: 7, of which 2 were waited for; matrix products, arithmetic and copies ran while one was open for 0% of the time, Pallas kernels for 14%

profile of v4, /device:TPU:30, one launch (start us, length us, event | category | flops | bytes accessed | tf_op | source)
XLA Modules:
  0.0 37.6 jit_solution(8546609377496784827)
XLA Ops:
  0.6 0.0 copy-start.2
  0.6 2.7 %chosen_rows.1 = (f32[528,128]{1,0:T(8,128)}, f32[8192,128]{1,0:T(8,128)}) custom-call(s32[32]{0:T(128)} %bitcast.23, f32[8192,128]{1,0:T(8,128)} %bitcast.15, f32[8192,128]{1,0:T(8,128)} %bitcast.18, f32[8192,1,128]{2,1,0:T(1,128)} %bitcast.16, f32[8192,1,128]{2,1,0:T(1,128)} %bitcast.19), custom_call_target="tpu_custom_call" | custom-call | tf_op jit(solution)/shard_map/chosen_rows/pallas_call | solution.py:134
  3.4 13.6 %all_to_all.5 = f32[16,33,1,128]{3,2,1,0:T(1,128)S(1)} all-to-all(f32[16,33,1,128]{3,2,1,0:T(1,128)} %bitcast.22), channel_id=1, replica_groups={{68,102,100,98,96,70,66,64,38,36,34,32,6,4,2,0},{69,103,101,99,97,71,67..., dimensions={0} | all-to-all | bytes 540672 | tf_op jit(solution)/shard_map/all_to_all | solution.py:257
  17.0 0.0 collective-permute-start
  17.0 0.0 copy-done.2
  17.0 1.1 %collective-permute-start.1 = (s32[1,64]{1,0:T(1,128)S(1)}, s32[1,64]{1,0:T(1,128)S(1)}, u32[]{:S(2)}, u32[]{:S(2)}) collective-permute-start(s32[1,64]{1,0:T(1,128)S(1)} %bitcast.11), channel_id=1, source_target_pairs={{0,8},{1,9},{2,10},{3,11},{4,12},{5,13},{6,14},{7,15},{8,0},{9,1},... | collective-permute-start | bytes 776 | tf_op jit(solution)/shard_map/ppermute | solution.py:246
  18.1 3.2 %collective-permute-start.2 = (s32[1,64]{1,0:T(1,128)S(1)}, s32[1,64]{1,0:T(1,128)S(1)}, u32[]{:S(2)}, u32[]{:S(2)}) collective-permute-start(s32[1,64]{1,0:T(1,128)S(1)} %bitcast.12), channel_id=1, source_target_pairs={{0,16},{1,17},{2,18},{3,19},{4,20},{5,21},{6,22},{7,23},{8,24},{9,... | collective-permute-start | bytes 776 | tf_op jit(solution)/shard_map/ppermute | solution.py:246
  21.3 0.4 %collective-permute-start.3 = (s32[1,64]{1,0:T(1,128)S(1)}, s32[1,64]{1,0:T(1,128)S(1)}, u32[]{:S(2)}, u32[]{:S(2)}) collective-permute-start(s32[1,64]{1,0:T(1,128)S(1)} %bitcast.13), channel_id=1, source_target_pairs={{0,24},{1,25},{2,26},{3,27},{4,28},{5,29},{6,30},{7,31},{8,16},{9,... | collective-permute-start | bytes 776 | tf_op jit(solution)/shard_map/ppermute | solution.py:246
  21.7 0.0 collective-permute-done.1.id1
  21.7 1.5 %collective-permute-done.2.id2 = s32[1,64]{1,0:T(1,128)S(1)} collective-permute-done((s32[1,64]{1,0:T(1,128)S(1)}, s32[1,64]{1,0:T(1,128)S(1)}, u32[]{:S(2)}, u32[]{:S(2)}) %collective-permute-start.2) | collective-permute-done | bytes 288 | tf_op jit(solution)/shard_map/ppermute | solution.py:246
  23.2 2.9 %collective-permute-done.3.id3 = s32[1,64]{1,0:T(1,128)S(1)} collective-permute-done((s32[1,64]{1,0:T(1,128)S(1)}, s32[1,64]{1,0:T(1,128)S(1)}, u32[]{:S(2)}, u32[]{:S(2)}) %collective-permute-start.3) | collective-permute-done | bytes 288 | tf_op jit(solution)/shard_map/ppermute | solution.py:246
  26.0 0.0 collective-permute-done.other
  26.0 0.6 %totals.1 = (f32[64,128]{1,0:T(8,128)S(1)}, f32[64,128]{1,0:T(8,128)S(1)}, f32[64,128]{1,0:T(8,128)S(1)}, f32[64,128]{1,0:T(8,128)S(1)}) custom-call(f32[528,128]{1,0:T(8,128)S(1)} %bitcast.10, f32[528,128]{1,0:T(8,128)S(1)} %collective-permute-done.other, s32[1,64]{1,0:T(1,128)S(1)} %bitcast.14, s32[1,64]{1,0:T(1,128)S(1)} %collective-permute-done.1.id1, ...), custom_call_target="tpu_custom_call" | custom-call | tf_op jit(solution)/shard_map/totals/pallas_call | solution.py:221
  26.7 0.1 collective-permute-start.4
  26.8 1.9 %collective-permute-start.5 = (f32[64,128]{1,0:T(8,128)S(1)}, f32[64,128]{1,0:T(8,128)S(1)}, u32[]{:S(2)}, u32[]{:S(2)}) collective-permute-start(f32[64,128]{1,0:T(8,128)S(1)} %get-tuple-element.15), channel_id=1, source_target_pairs={{0,16},{1,17},{2,18},{3,19},{4,20},{5,21},{6,22},{7,23},{8,24},{9,... | collective-permute-start | bytes 98312 | tf_op jit(solution)/shard_map/ppermute | solution.py:246
  28.7 2.8 %collective-permute-start.6 = (f32[64,128]{1,0:T(8,128)S(1)}, f32[64,128]{1,0:T(8,128)S(1)}, u32[]{:S(2)}, u32[]{:S(2)}) collective-permute-start(f32[64,128]{1,0:T(8,128)S(1)} %get-tuple-element.16), channel_id=1, source_target_pairs={{0,24},{1,25},{2,26},{3,27},{4,28},{5,29},{6,30},{7,31},{8,16},{9,... | collective-permute-start | bytes 98312 | tf_op jit(solution)/shard_map/ppermute | solution.py:246
  31.5 0.0 copy-start
  31.5 0.0 copy-start.1
  31.5 5.4 %remainder.1 = f32[8192,128]{1,0:T(8,128)} custom-call(s32[32]{0:T(128)} %bitcast.24, f32[8192,128]{1,0:T(8,128)} %bitcast.17, f32[8192,128]{1,0:T(8,128)} %bitcast.20, f32[8192,128]{1,0:T(8,128)} %get-tuple-element.11.begun), custom_call_target="tpu_custom_call", output_to_operand_aliasing={{}: (3, {})} | custom-call | flops 40000000 | bytes 12582912 | tf_op jit(solution)/shard_map/remainder/pallas_call | solution.py:172
  36.9 0.0 collective-permute-done.4.b
  36.9 0.0 collective-permute-done.5.c
  36.9 0.0 collective-permute-done.6.d
  36.9 0.0 copy-done
  36.9 0.0 copy-done.1
  37.0 0.6 %update.1 = (f32[64,128]{1,0:T(8,128)}, f32[64,128]{1,0:T(8,128)}) custom-call(f32[64,128]{1,0:T(8,128)S(1)} %copy-done, f32[64,128]{1,0:T(8,128)S(1)} %copy-done.1, f32[64,128]{1,0:T(8,128)S(1)} %get-tuple-element.13.a, f32[64,128]{1,0:T(8,128)S(1)} %collective-permute-done.4.b, f32[64,128]{1,0:T(8,128)S(1)} %collective-permute-done.5.c, ...), custom_call_target="tpu_custom_call" | custom-call | tf_op jit(solution)/shard_map/update/pallas_call | solution.py:237
Async XLA Ops:
  0.6 16.3 %copy-start.2 = (s32[64]{0:T(128)S(1)}, s32[64]{0:T(128)}, u32[]{:S(2)}) copy-start(s32[64]{0:T(128)} %param.9) | copy-start | bytes 772
  17.0 9.1 %collective-permute-start = (f32[528,128]{1,0:T(8,128)S(1)}, f32[528,128]{1,0:T(8,128)S(1)}, u32[]{:S(2)}, u32[]{:S(2)}) collective-permute-start(f32[528,128]{1,0:T(8,128)S(1)} %bitcast.9), channel_id=1, source_target_pairs={{0,1},{1,0},{2,3},{3,2},{4,5},{5,4},{6,7},{7,6},{8,9},{9,8},{10,11... | collective-permute-start | bytes 811016 | tf_op jit(solution)/shard_map/ppermute | solution.py:261
  17.0 4.7 %collective-permute-start.1 = (s32[1,64]{1,0:T(1,128)S(1)}, s32[1,64]{1,0:T(1,128)S(1)}, u32[]{:S(2)}, u32[]{:S(2)}) collective-permute-start(s32[1,64]{1,0:T(1,128)S(1)} %bitcast.11), channel_id=1, source_target_pairs={{0,8},{1,9},{2,10},{3,11},{4,12},{5,13},{6,14},{7,15},{8,0},{9,1},... | collective-permute-start | bytes 776 | tf_op jit(solution)/shard_map/ppermute | solution.py:246
  18.1 5.1 %collective-permute-start.2 = (s32[1,64]{1,0:T(1,128)S(1)}, s32[1,64]{1,0:T(1,128)S(1)}, u32[]{:S(2)}, u32[]{:S(2)}) collective-permute-start(s32[1,64]{1,0:T(1,128)S(1)} %bitcast.12), channel_id=1, source_target_pairs={{0,16},{1,17},{2,18},{3,19},{4,20},{5,21},{6,22},{7,23},{8,24},{9,... | collective-permute-start | bytes 776 | tf_op jit(solution)/shard_map/ppermute | solution.py:246
  21.3 4.8 %collective-permute-start.3 = (s32[1,64]{1,0:T(1,128)S(1)}, s32[1,64]{1,0:T(1,128)S(1)}, u32[]{:S(2)}, u32[]{:S(2)}) collective-permute-start(s32[1,64]{1,0:T(1,128)S(1)} %bitcast.13), channel_id=1, source_target_pairs={{0,24},{1,25},{2,26},{3,27},{4,28},{5,29},{6,30},{7,31},{8,16},{9,... | collective-permute-start | bytes 776 | tf_op jit(solution)/shard_map/ppermute | solution.py:246
  26.7 10.2 %collective-permute-start.4 = (f32[64,128]{1,0:T(8,128)S(1)}, f32[64,128]{1,0:T(8,128)S(1)}, u32[]{:S(2)}, u32[]{:S(2)}) collective-permute-start(f32[64,128]{1,0:T(8,128)S(1)} %get-tuple-element.14), channel_id=1, source_target_pairs={{0,8},{1,9},{2,10},{3,11},{4,12},{5,13},{6,14},{7,15},{8,0},{9,1},... | collective-permute-start | bytes 98312 | tf_op jit(solution)/shard_map/ppermute | solution.py:246
  26.8 10.1 %collective-permute-start.5 = (f32[64,128]{1,0:T(8,128)S(1)}, f32[64,128]{1,0:T(8,128)S(1)}, u32[]{:S(2)}, u32[]{:S(2)}) collective-permute-start(f32[64,128]{1,0:T(8,128)S(1)} %get-tuple-element.15), channel_id=1, source_target_pairs={{0,16},{1,17},{2,18},{3,19},{4,20},{5,21},{6,22},{7,23},{8,24},{9,... | collective-permute-start | bytes 98312 | tf_op jit(solution)/shard_map/ppermute | solution.py:246
  28.7 8.3 %collective-permute-start.6 = (f32[64,128]{1,0:T(8,128)S(1)}, f32[64,128]{1,0:T(8,128)S(1)}, u32[]{:S(2)}, u32[]{:S(2)}) collective-permute-start(f32[64,128]{1,0:T(8,128)S(1)} %get-tuple-element.16), channel_id=1, source_target_pairs={{0,24},{1,25},{2,26},{3,27},{4,28},{5,29},{6,30},{7,31},{8,16},{9,... | collective-permute-start | bytes 98312 | tf_op jit(solution)/shard_map/ppermute | solution.py:246
  31.5 5.5 %copy-start = (f32[64,128]{1,0:T(8,128)S(1)}, f32[64,128]{1,0:T(8,128)}, u32[]{:S(2)}) copy-start(f32[64,128]{1,0:T(8,128)} %momentum.1) | copy-start | bytes 98308
  31.5 5.5 %copy-start.1 = (f32[64,128]{1,0:T(8,128)S(1)}, f32[64,128]{1,0:T(8,128)}, u32[]{:S(2)}) copy-start(f32[64,128]{1,0:T(8,128)} %params.1) | copy-start | bytes 98308
